TPU v7x, 32 devices: a whole 2x2x4 slice. The times are simulated.
32 devices in a mesh: sub: 8 (over z, y), grp: 4 (over x, core).
Axes of the slice: x: 2, y: 2, z: 4, core: 2. Of those that a mesh axis runs over, the one named last changes fastest.
Arguments:
- rr_inverse: float32 [64, 512, 512], P(('sub', 'grp')), may hold values from -4 to 4, as said below
- corner_modes: float32 [64, 64, 512], P(('sub', 'grp')), may hold values from -0.5 to 0.5
- coarse_inverse: float32 [2048, 2048], P(('sub', 'grp')), may hold values from -1 to 1, as said below
- inertia: float32 [64, 512], P(('sub', 'grp')), may hold values from 0.5 to 2
- disp_now: float32 [8, 64, 512], P(None, ('sub', 'grp')), may hold values from -4 to 4
- vel_now: float32 [8, 64, 512], P(None, ('sub', 'grp')), may hold values from -4 to 4
- acc_now: float32 [8, 64, 512], P(None, ('sub', 'grp')), may hold values from -8 to 8
- load_next: float32 [8, 64, 512], P(None, ('sub', 'grp')), may hold values from -10 to 10
- basis_rows: float32 [32768, 256], P(('sub', 'grp')), may hold values from -0.03125 to 0.03125
- piece_owner: int32 [32], replicated, may hold values from 0 to 31, each once
Outputs:
- disp_new: float32 [8, 64, 512], P(None, ('sub', 'grp'))
- vel_new: float32 [8, 64, 512], P(None, ('sub', 'grp'))
- projection: float32 [256, 8], replicated
- r_factor: float32 [8, 8], replicated
- new_columns: float32 [8, 32768], P(None, ('sub', 'grp'))
Inputs may be any that keep to these rules, and one draw needn't show every extreme that they name: piece_owner is a permutation. `rr_inverse`: each of the 64 blocks is symmetric positive definite. `coarse_inverse`: symmetric positive definite.
All inputs are finite; a program needn't handle non-finite values.
Results may differ from a plain program's by a relative error of at most 0.00018.
Values sent between devices are 32-bit elements; how exact they have to be, the bound alone decides.
A program may use at most 64 MiB of HBM per device.

v0:
```python
import math
import jax
import jax.numpy as jnp
from jax import lax
from jax.sharding import PartitionSpec as P

NC = 32
ITERS = 2
NI = 128
highest = lax.Precision.HIGHEST
time_step = 0.5
newmark_beta = 0.25
newmark_gamma = 0.5


def shifted(array, axis, by):
    count = lax.axis_size(axis)
    return lax.ppermute(array, axis, [(i, (i + by) % count) for i in range(count)])


def contract(segment, matrix_rows):
    return lax.dot_general(segment, matrix_rows, (((1,), (1,)), ((), ())), precision=highest)


def shards(
    rr_inverse,
    corner_modes,
    coarse_inverse,
    inertia,
    disp_now,
    vel_now,
    acc_now,
    load_next,
    basis_rows,
    piece_owner,
):
    case_count, sub_count, unknowns = disp_now.shape
    coarse_total = coarse_inverse.shape[1]
    row_count = sub_count * NC
    shifted_rows = jnp.roll(coarse_inverse, NC, axis=1)
    coarse_pairs = jnp.concatenate(
        [
            shifted_rows.reshape(row_count, coarse_total // NC, NC),
            coarse_inverse.reshape(row_count, coarse_total // NC, NC),
        ],
        axis=2,
    ).reshape(row_count, 2 * coarse_total)

    def apply_green(field):
        local_part = jnp.einsum("jab,cjb->cja", rr_inverse, field, precision=highest)
        corner_terms = jnp.einsum("jmb,cjb->cjm", corner_modes, field, precision=highest)
        flat_terms = corner_terms.reshape(case_count, sub_count * 2 * NC)
        owned_sums = contract(
            lax.all_gather(flat_terms, ("sub", "grp"), axis=1, tiled=True), coarse_pairs
        )
        previous = shifted(owned_sums[:, row_count - NC :], ("sub", "grp"), 1)
        owned_blocks = owned_sums.reshape(case_count, sub_count, NC)
        left_values = jnp.concatenate(
            [previous.reshape(case_count, 1, NC), owned_blocks[:, :-1]], axis=1
        )
        coarse_values = jnp.concatenate([left_values, owned_blocks], axis=2)
        return local_part + jnp.einsum(
            "jmb,cjm->cjb", corner_modes, coarse_values, precision=highest
        )

    def interface_jump(field):
        following = shifted(field[:, :1, :NI], ("sub", "grp"), -1)
        first_parts = jnp.concatenate([field[:, 1:, :NI], following], axis=1)
        return field[:, :, unknowns - NI :] - first_parts

    def squared_norm(values):
        return lax.psum(jnp.sum(values * values, axis=(1, 2)), ("sub", "grp"))

    right_side = load_next + inertia[None] * (
        disp_now + time_step * vel_now + (0.5 - newmark_beta) * time_step * time_step * acc_now
    )
    green_rhs = apply_green(right_side)
    residual = interface_jump(green_rhs)
    carried = green_rhs
    direction = residual
    norm_now = squared_norm(residual)
    for iteration in range(ITERS):
        earlier = shifted(direction[:, -1:], ("sub", "grp"), 1)
        left_parts = jnp.concatenate([earlier, direction[:, :-1]], axis=1)
        middle = jnp.zeros((case_count, sub_count, unknowns - 2 * NI), jnp.float32)
        image_field = apply_green(jnp.concatenate([-left_parts, middle, direction], axis=2))
        image = interface_jump(image_field)
        curvature = lax.psum(jnp.sum(direction * image, axis=(1, 2)), ("sub", "grp"))
        alpha = (norm_now / curvature)[:, None, None]
        carried = carried - alpha * image_field
        residual = residual - alpha * image
        if iteration + 1 < ITERS:
            norm_next = squared_norm(residual)
            direction = residual + (norm_next / norm_now)[:, None, None] * direction
            norm_now = norm_next
    accel_new = (
        (carried - disp_now) / (newmark_beta * time_step * time_step)
        - vel_now / (newmark_beta * time_step)
        - (0.5 / newmark_beta - 1.0) * acc_now
    )
    vel_new = vel_now + time_step * ((1.0 - newmark_gamma) * acc_now + newmark_gamma * accel_new)
    piece_total = lax.axis_size(("sub", "grp"))
    piece_rows = unknowns // piece_total
    inverse = (
        jnp.zeros((piece_total,), jnp.int32)
        .at[piece_owner]
        .set(jnp.arange(piece_total, dtype=jnp.int32))
    )
    outgoing = carried.reshape(case_count, sub_count, piece_total, piece_rows)[:, :, inverse, :]
    outgoing = jnp.transpose(outgoing, (0, 2, 1, 3)).reshape(
        case_count, piece_total * sub_count * piece_rows
    )
    received = lax.all_to_all(outgoing, ("sub", "grp"), split_axis=1, concat_axis=1, tiled=True)
    projection_part = lax.dot_general(
        basis_rows, received, (((0,), (1,)), ((), ())), precision=highest
    )
    projection = lax.psum(projection_part, ("sub", "grp"))
    remainder = received - lax.dot_general(
        projection, basis_rows, (((0,), (1,)), ((), ())), precision=highest
    )
    gram_local = lax.dot_general(remainder, remainder, (((1,), (1,)), ((), ())), precision=highest)
    lower = jnp.linalg.cholesky(lax.psum(gram_local, ("sub", "grp")))
    scale_rows = math.sqrt(received.shape[1] * piece_total)
    new_columns = jax.scipy.linalg.solve_triangular(lower, remainder, lower=True) * scale_rows
    r_factor = lower.T / scale_rows
    return (carried, vel_new, projection, r_factor, new_columns)


def solution(mesh):
    return jax.shard_map(
        shards,
        mesh=mesh,
        in_specs=(
            P(("sub", "grp"), None, None),
            P(("sub", "grp"), None, None),
            P(("sub", "grp"), None),
            P(("sub", "grp"), None),
            P(None, ("sub", "grp"), None),
            P(None, ("sub", "grp"), None),
            P(None, ("sub", "grp"), None),
            P(None, ("sub", "grp"), None),
            P(("sub", "grp"), None),
            P(),
        ),
        out_specs=(
            P(None, ("sub", "grp"), None),
            P(None, ("sub", "grp"), None),
            P(),
            P(),
            P(None, ("sub", "grp")),
        ),
        check_vma=False,
    )
```

profile of v0, /device:TPU:0, one launch (start us, length us, event | category | flops | bytes accessed | tf_op | source)
XLA Modules:
  0.0 396.2 jit_solution(17063526511338648422)
XLA Ops:
  0.7 1.5 copy.65
  2.2 1.1 slice.101
  3.4 0.3 convolution_bitcast_fusion.3
  3.8 43.6 %all_gather.9 = f32[8,4096]{1,0:T(8,128)S(1)} all-gather(f32[8,128]{1,0:T(8,128)S(1)} %reshape.67), channel_id=1, replica_groups=mesh['sub'=8,'grp'=4] {'sub','grp'}, dimensions={1}, use_global_device_ids=true | all-gather | bytes 135168 | tf_op jit(solution)/shard_map/all_gather | solution.py:54
  47.4 1.3 pad_maximum_fusion.1
  48.7 0.2 pad_maximum_fusion
  48.9 1.3 copy-done.1
  50.2 1.1 fusion.49
  51.4 0.4 collective-permute-start
  51.8 1.8 fusion.10
  53.7 4.4 %collective-permute-done = f32[8,32]{1,0:T(8,128)S(1)} collective-permute-done((f32[8,32]{1,0:T(8,128)S(1)}, f32[8,32]{1,0:T(8,128)S(1)}, u32[]{:S(2)}, u32[]{:S(2)}) %collective-permute-start) | collective-permute-done | bytes 1056 | tf_op jit(solution)/shard_map/ppermute | solution.py:18
  58.1 0.3 fusion.2
  58.4 0.7 collective-permute-start.1
  59.0 1.3 collective-permute-done.1
  60.4 6.6 %collective-permute-done.2 = f32[8,1,128]{2,0,1:T(8,128)S(1)} collective-permute-done((f32[8,1,128]{2,0,1:T(8,128)S(1)}, f32[8,1,128]{2,0,1:T(8,128)S(1)}, u32[]{:S(2)}, u32[]{:S(2)}) %collective-permute-start.2) | collective-permute-done | bytes 4128 | tf_op jit(solution)/shard_map/ppermute | solution.py:18
  67.0 0.3 convolution_bitcast_fusion.2
  67.4 36.7 %all_gather.10 = f32[8,4096]{1,0:T(8,128)S(1)} all-gather(f32[8,128]{1,0:T(8,128)S(1)} %reshape.73), channel_id=1, replica_groups=mesh['sub'=8,'grp'=4] {'sub','grp'}, dimensions={1}, use_global_device_ids=true | all-gather | bytes 135168 | tf_op jit(solution)/shard_map/all_gather | solution.py:54
  104.1 2.7 fusion.50
  106.9 0.4 collective-permute-start.3
  107.2 1.8 fusion.5
  109.1 4.4 %collective-permute-done.3 = f32[8,32]{1,0:T(8,128)S(1)} collective-permute-done((f32[8,32]{1,0:T(8,128)S(1)}, f32[8,32]{1,0:T(8,128)S(1)}, u32[]{:S(2)}, u32[]{:S(2)}) %collective-permute-start.3) | collective-permute-done | bytes 1056 | tf_op jit(solution)/shard_map/ppermute | solution.py:18
  113.5 0.3 fusion.1
  113.8 0.7 collective-permute-start.4
  114.5 1.3 collective-permute-done.4
  115.8 0.1 multiply_reduce_fusion.1
  116.0 38.1 %all-reduce = (f32[8]{0:T(128)S(1)}, f32[8]{0:T(128)S(1)}) all-reduce(f32[8]{0:T(128)S(1)} %get-tuple-element.21, f32[8]{0:T(128)S(1)} %get-tuple-element.20), channel_id=1, replica_groups=mesh['sub'=8,'grp'=4] {'sub','grp'}, use_global_device_ids=true, to_apply=%region_1.2 | all-reduce | flops 16 | bytes 128 | tf_op jit(solution)/shard_map/psum | solution.py:72
  154.1 0.2 multiply_reduce_fusion
  154.3 42.1 %psum.44 = f32[8]{0:T(128)S(1)} all-reduce(f32[8]{0:T(128)S(1)} %multiply_reduce_fusion), channel_id=1, replica_groups=mesh['sub'=8,'grp'=4] {'sub','grp'}, use_global_device_ids=true, to_apply=%region_5.6 | all-reduce | flops 8 | bytes 64 | tf_op jit(solution)/shard_map/psum | solution.py:72
  196.5 0.7 scatter_custom_fusion
  197.2 5.9 %collective-permute-done.5 = f32[8,1,128]{2,0,1:T(8,128)S(1)} collective-permute-done((f32[8,1,128]{2,0,1:T(8,128)S(1)}, f32[8,1,128]{2,0,1:T(8,128)S(1)}, u32[]{:S(2)}, u32[]{:S(2)}) %collective-permute-start.5) | collective-permute-done | bytes 4128 | tf_op jit(solution)/shard_map/ppermute | solution.py:18
  203.1 0.3 convolution_bitcast_fusion.1
  203.5 36.7 %all_gather.11 = f32[8,4096]{1,0:T(8,128)S(1)} all-gather(f32[8,128]{1,0:T(8,128)S(1)} %reshape.76), channel_id=1, replica_groups=mesh['sub'=8,'grp'=4] {'sub','grp'}, dimensions={1}, use_global_device_ids=true | all-gather | bytes 135168 | tf_op jit(solution)/shard_map/all_gather | solution.py:54
  240.2 2.7 fusion.51
  242.9 0.5 collective-permute-start.6
  243.4 2.5 fusion.6
  246.0 3.7 collective-permute-done.6
  249.7 1.0 fusion
  250.8 1.4 collective-permute-start.7
  252.2 1.3 collective-permute-done.7
  253.5 0.1 fusion.17
  253.6 38.1 %psum.45 = f32[8]{0:T(128)S(1)} all-reduce(f32[8]{0:T(128)S(1)} %fusion.17), channel_id=1, replica_groups=mesh['sub'=8,'grp'=4] {'sub','grp'}, use_global_device_ids=true, to_apply=%region_7.8 | all-reduce | flops 8 | bytes 64 | tf_op jit(solution)/shard_map/psum | solution.py:88
  291.7 1.5 fusion.4
  293.2 0.1 reshape.79
  293.3 0.8 copy.81
  294.2 1.5 gather_fusion
  295.7 0.2 copy.82
  296.0 0.7 reshape.100
  296.7 6.5 %all-to-all-start = ((f32[32,1,256]{2,1,0:T(1,128)}), f32[32,1,256]{2,1,0:T(1,128)S(1)}, u32[]{:S(2)}, u32[]{:S(2)}) async-start(f32[32,1,256]{2,1,0:T(1,128)} %reshape.100), calls=%async_computation | async-start | bytes 65536 | tf_op jit(solution)/shard_map/all_to_all | solution.py:113
  303.2 1.4 copy.88
  304.6 1.4 copy.89
  306.0 4.5 %all-to-all-done = f32[32,1,256]{2,1,0:T(1,128)S(1)} async-done(((f32[32,1,256]{2,1,0:T(1,128)}), f32[32,1,256]{2,1,0:T(1,128)S(1)}, u32[]{:S(2)}, u32[]{:S(2)}) %all-to-all-start) | async-done | bytes 32800 | tf_op jit(solution)/shard_map/all_to_all | solution.py:113
  310.5 0.5 broadcast.116
  311.0 0.7 reduce.6
  311.9 0.5 convolution_bitcast_fusion
  312.5 38.3 %psum.46 = f32[256,8]{0,1:T(8,128)S(1)} all-reduce(f32[256,8]{0,1:T(8,128)S(1)} %convolution_bitcast_fusion), channel_id=1, replica_groups=mesh['sub'=8,'grp'=4] {'sub','grp'}, use_global_device_ids=true, to_apply=%region_9.10 | all-reduce | flops 2048 | bytes 16384 | tf_op jit(solution)/shard_map/psum | solution.py:117
  350.7 1.0 convolution_subtract_fusion
  351.7 0.2 fusion.52
  351.8 40.1 %psum.47 = f32[8,8]{0,1:T(8,128)S(1)} all-reduce(f32[8,8]{0,1:T(8,128)S(1)} %fusion.52), channel_id=1, replica_groups=mesh['sub'=8,'grp'=4] {'sub','grp'}, use_global_device_ids=true, to_apply=%region_10.11 | all-reduce | flops 64 | bytes 512 | tf_op jit(solution)/shard_map/psum | solution.py:122
  392.0 0.7 cholesky.18
  392.7 0.6 compare_reduce_fusion
  393.4 0.6 select_bitcast_fusion
  394.0 0.6 custom-call.7
  394.7 0.9 convolution_multiply_fusion
  395.5 0.7 copy.90
  (70 shorter events, 1.5 us)
Async XLA Ops:
  0.6 51.1 %copy-start = (f32[2,512,512]{2,1,0:T(8,128)S(1)}, f32[2,512,512]{2,1,0:T(8,128)}, u32[]{:S(2)}) copy-start(f32[2,512,512]{2,1,0:T(8,128)} %param.10) | copy-start | bytes 6291460
  0.6 2.7 copy-start.6
  0.7 2.7 copy-start.7
  0.7 2.6 copy-start.5
  0.7 2.7 copy-start.2
  2.2 1.1 copy-start.9
  2.2 1.1 copy-start.10
  48.9 1.4 copy-start.1
  51.4 6.7 %collective-permute-start = (f32[8,32]{1,0:T(8,128)S(1)}, f32[8,32]{1,0:T(8,128)S(1)}, u32[]{:S(2)}, u32[]{:S(2)}) collective-permute-start(f32[8,32]{1,0:T(8,128)S(1)} %slice.79), channel_id=1, source_target_pairs={{0,1},{1,2},{2,3},{3,4},{4,5},{5,6},{6,7},{7,8},{8,9},{9,10},{10,1... | collective-permute-start | bytes 3080 | tf_op jit(solution)/shard_map/ppermute | solution.py:18
  58.4 2.0 collective-permute-start.1
  60.4 6.6 %collective-permute-start.2 = (f32[8,1,128]{2,0,1:T(8,128)S(1)}, f32[8,1,128]{2,0,1:T(8,128)S(1)}, u32[]{:S(2)}, u32[]{:S(2)}) collective-permute-start(f32[8,1,128]{2,0,1:T(8,128)S(1)} %get-tuple-element.34), channel_id=1, source_target_pairs={{0,1},{1,2},{2,3},{3,4},{4,5},{5,6},{6,7},{7,8},{8,9},{9,10},{10,1... | collective-permute-start | bytes 12296 | tf_op jit(solution)/shard_map/ppermute | solution.py:18
  104.1 92.4 %copy-start.11 = (s32[32]{0:T(128)S(1)}, s32[32]{0:T(128)}, u32[]{:S(2)}) copy-start(s32[32]{0:T(128)} %param.19) | copy-start | bytes 388
  106.9 6.6 %collective-permute-start.3 = (f32[8,32]{1,0:T(8,128)S(1)}, f32[8,32]{1,0:T(8,128)S(1)}, u32[]{:S(2)}, u32[]{:S(2)}) collective-permute-start(f32[8,32]{1,0:T(8,128)S(1)} %slice.86), channel_id=1, source_target_pairs={{0,1},{1,2},{2,3},{3,4},{4,5},{5,6},{6,7},{7,8},{8,9},{9,10},{10,1... | collective-permute-start | bytes 3080 | tf_op jit(solution)/shard_map/ppermute | solution.py:18
  113.8 2.0 collective-permute-start.4
  196.4 6.6 %collective-permute-start.5 = (f32[8,1,128]{2,0,1:T(8,128)S(1)}, f32[8,1,128]{2,0,1:T(8,128)S(1)}, u32[]{:S(2)}, u32[]{:S(2)}) collective-permute-start(f32[8,1,128]{2,0,1:T(8,128)S(1)} %get-tuple-element.32), channel_id=1, source_target_pairs={{0,1},{1,2},{2,3},{3,4},{4,5},{5,6},{6,7},{7,8},{8,9},{9,10},{10,1... | collective-permute-start | bytes 12296 | tf_op jit(solution)/shard_map/ppermute | solution.py:18
  242.9 6.8 %collective-permute-start.6 = (f32[8,32]{1,0:T(8,128)S(1)}, f32[8,32]{1,0:T(8,128)S(1)}, u32[]{:S(2)}, u32[]{:S(2)}) collective-permute-start(f32[8,32]{1,0:T(8,128)S(1)} %slice.93), channel_id=1, source_target_pairs={{0,1},{1,2},{2,3},{3,4},{4,5},{5,6},{6,7},{7,8},{8,9},{9,10},{10,1... | collective-permute-start | bytes 3080 | tf_op jit(solution)/shard_map/ppermute | solution.py:18
  245.9 66.0 %copy-start.3 = (f32[1024,256]{1,0:T(8,128)S(1)}, f32[1024,256]{1,0:T(8,128)}, u32[]{:S(2)}) copy-start(f32[1024,256]{1,0:T(8,128)} %param.18) | copy-start | bytes 3145732
  250.8 2.7 collective-permute-start.7
  293.2 2.5 copy-start.4
  296.7 13.7 %all-to-all-start = ((f32[32,1,256]{2,1,0:T(1,128)}), f32[32,1,256]{2,1,0:T(1,128)S(1)}, u32[]{:S(2)}, u32[]{:S(2)}) async-start(f32[32,1,256]{2,1,0:T(1,128)} %reshape.100), calls=%async_computation | async-start | bytes 65536 | tf_op jit(solution)/shard_map/all_to_all | solution.py:113
  350.7 45.5 %copy-start.8 = (f32[256,8]{0,1:T(8,128)}, f32[256,8]{0,1:T(8,128)S(1)}, u32[]{:S(2)}) copy-start(f32[256,8]{0,1:T(8,128)S(1)} %psum.46) | copy-start | bytes 24580
where the time goes:
time: 397 us; the launch traced here: 396 us
  blocking collectives  314 us (79%)
  waiting for transfers between devices  33.4 us (8%)
  matrix products  17.6 us (4%)
  local copies, waits for them, and re-layouts  13.2 us (3%)
  starting transfers between devices  10.5 us (3%)
  other arithmetic  6.97 us (2%)
    all_gather x3, blocking collectives, apply_green(): lax.all_gather(flat_terms, ('sub', 'grp'), axis=1, tiled=True)  117 us
    psum x2, blocking collectives, squared_norm(): return lax.psum(jnp.sum(values * values, axis=(1, 2)), ('sub', 'grp'))  80.2 us
    psum x1, blocking collectives, shards(): lower = jnp.linalg.cholesky(lax.psum(gram_local, ('sub', 'grp')))  40.1 us
    psum x1, blocking collectives, shards(): projection = lax.psum(projection_part, ('sub', 'grp'))  38.3 us
    psum x1, blocking collectives, shards(): lax.psum(jnp.sum(direction * image, axis=(1, 2)), ('sub', 'grp'))  38.1 us
    ppermute x8, waiting for transfers between devices, shifted(): lax.ppermute(array, axis, [(i, (i + by) % count) for i in range(count)])  29 us
  transfers between devices with their start and end apart: 9, of which 9 were waited for; matrix products, arithmetic and copies ran while one was open for 2% of the time, Pallas kernels for 0%

commit v1 on v0

--- a/solution.py
+++ b/solution.py
@@ -1,8 +1,10 @@
+import functools
 import math
 import jax
 import jax.numpy as jnp
 from jax import lax
 from jax.sharding import PartitionSpec as P
+from jax.lax import psum
 
 NC = 32
 ITERS = 2
@@ -11,6 +13,15 @@
 time_step = 0.5
 newmark_beta = 0.25
 newmark_gamma = 0.5
+
+
+def ends_derive(my_data, comm_axis, link_axis):
+    for dd in (comm_axis, link_axis):
+        my_data = psum(my_data, dd)
+    return my_data
+
+
+_choose_values = functools.partial(ends_derive, comm_axis="grp", link_axis="sub")
 
 
 def shifted(array, axis, by):
@@ -85,7 +96,7 @@
         middle = jnp.zeros((case_count, sub_count, unknowns - 2 * NI), jnp.float32)
         image_field = apply_green(jnp.concatenate([-left_parts, middle, direction], axis=2))
         image = interface_jump(image_field)
-        curvature = lax.psum(jnp.sum(direction * image, axis=(1, 2)), ("sub", "grp"))
+        curvature = _choose_values(jnp.sum(direction * image, axis=(1, 2)))
         alpha = (norm_now / curvature)[:, None, None]
         carried = carried - alpha * image_field
         residual = residual - alpha * image

time: 397 us -> 411 us (1.035)
  blocking collectives: 314 us -> 331 us
    psum x1 -> x4, blocking collectives: 38.1 us -> 57.3 us  [ends_derive(): my_data = psum(my_data, dd)]
where the time goes in v1:
time: 411 us; the launch traced here: 410 us
  blocking collectives  331 us (81%)
  waiting for transfers between devices  33.5 us (8%)
  matrix products  17.6 us (4%)
  local copies, waits for them, and re-layouts  13.2 us (3%)
  other arithmetic  6.97 us (2%)
  starting transfers between devices  6.59 us (2%)
    all_gather x3, blocking collectives, apply_green(): lax.all_gather(flat_terms, ('sub', 'grp'), axis=1, tiled=True)  118 us
    psum x2, blocking collectives, squared_norm(): return lax.psum(jnp.sum(values * values, axis=(1, 2)), ('sub', 'grp'))  78 us
    psum x4, blocking collectives, ends_derive(): my_data = psum(my_data, dd)  57.3 us
    psum x1, blocking collectives, shards(): lower = jnp.linalg.cholesky(lax.psum(gram_local, ('sub', 'grp')))  40.1 us
    psum x1, blocking collectives, shards(): projection = lax.psum(projection_part, ('sub', 'grp'))  38.3 us
    ppermute x8, waiting for transfers between devices, shifted(): lax.ppermute(array, axis, [(i, (i + by) % count) for i in range(count)])  29 us
  transfers between devices with their start and end apart: 9, of which 9 were waited for; matrix products, arithmetic and copies ran while one was open for 2% of the time, Pallas kernels for 0%

profile of v1, /device:TPU:0, one launch (start us, length us, event | category | flops | bytes accessed | tf_op | source)
XLA Modules:
  0.0 410.0 jit_solution(17074023163622557388)
XLA Ops:
  0.7 1.5 copy.65
  2.2 1.1 slice.101
  3.4 0.3 convolution_bitcast_fusion.3
  3.8 43.6 %all_gather.9 = f32[8,4096]{1,0:T(8,128)S(1)} all-gather(f32[8,128]{1,0:T(8,128)S(1)} %reshape.67), channel_id=1, replica_groups=mesh['sub'=8,'grp'=4] {'sub','grp'}, dimensions={1}, use_global_device_ids=true | all-gather | bytes 135168 | tf_op jit(solution)/shard_map/all_gather | solution.py:65
  47.4 1.3 pad_maximum_fusion.1
  48.7 0.2 pad_maximum_fusion
  48.9 1.3 copy-done.1
  50.2 1.1 fusion.49
  51.4 0.4 collective-permute-start
  51.8 1.8 fusion.10
  53.7 4.4 %collective-permute-done = f32[8,32]{1,0:T(8,128)S(1)} collective-permute-done((f32[8,32]{1,0:T(8,128)S(1)}, f32[8,32]{1,0:T(8,128)S(1)}, u32[]{:S(2)}, u32[]{:S(2)}) %collective-permute-start) | collective-permute-done | bytes 1056 | tf_op jit(solution)/shard_map/ppermute | solution.py:29
  58.1 0.3 fusion.2
  58.4 0.7 collective-permute-start.1
  59.0 1.3 collective-permute-done.1
  60.4 6.6 %collective-permute-done.2 = f32[8,1,128]{2,0,1:T(8,128)S(1)} collective-permute-done((f32[8,1,128]{2,0,1:T(8,128)S(1)}, f32[8,1,128]{2,0,1:T(8,128)S(1)}, u32[]{:S(2)}, u32[]{:S(2)}) %collective-permute-start.2) | collective-permute-done | bytes 4128 | tf_op jit(solution)/shard_map/ppermute | solution.py:29
  67.0 0.3 convolution_bitcast_fusion.2
  67.4 36.7 %all_gather.10 = f32[8,4096]{1,0:T(8,128)S(1)} all-gather(f32[8,128]{1,0:T(8,128)S(1)} %reshape.73), channel_id=1, replica_groups=mesh['sub'=8,'grp'=4] {'sub','grp'}, dimensions={1}, use_global_device_ids=true | all-gather | bytes 135168 | tf_op jit(solution)/shard_map/all_gather | solution.py:65
  104.1 2.7 fusion.50
  106.9 0.4 collective-permute-start.3
  107.2 1.8 fusion.5
  109.1 4.4 %collective-permute-done.3 = f32[8,32]{1,0:T(8,128)S(1)} collective-permute-done((f32[8,32]{1,0:T(8,128)S(1)}, f32[8,32]{1,0:T(8,128)S(1)}, u32[]{:S(2)}, u32[]{:S(2)}) %collective-permute-start.3) | collective-permute-done | bytes 1056 | tf_op jit(solution)/shard_map/ppermute | solution.py:29
  113.5 0.3 fusion.1
  113.8 0.7 collective-permute-start.4
  114.5 1.3 collective-permute-done.4
  116.0 5.8 %psum.57 = f32[8]{0:T(128)S(1)} all-reduce(f32[8]{0:T(128)S(1)} %get-tuple-element.20), channel_id=1, replica_groups=mesh['sub'=8,'grp'=4] {'grp'}, use_global_device_ids=true, to_apply=%region_3.4 | all-reduce | flops 8 | bytes 64 | tf_op jit(solution)/shard_map/psum | solution.py:20
  121.7 22.9 %psum.58 = f32[8]{0:T(128)S(1)} all-reduce(f32[8]{0:T(128)S(1)} %psum.57), channel_id=1, replica_groups=mesh['sub'=8,'grp'=4] {'sub'}, use_global_device_ids=true, to_apply=%region_4.5 | all-reduce | flops 8 | bytes 64 | tf_op jit(solution)/shard_map/psum | solution.py:20
  144.6 36.8 %psum.56 = f32[8]{0:T(128)S(1)} all-reduce(f32[8]{0:T(128)S(1)} %get-tuple-element.21), channel_id=1, replica_groups=mesh['sub'=8,'grp'=4] {'sub','grp'}, use_global_device_ids=true, to_apply=%region_1.2 | all-reduce | flops 8 | bytes 64 | tf_op jit(solution)/shard_map/psum | solution.py:83
  181.4 0.2 multiply_reduce_fusion
  181.6 41.2 %psum.59 = f32[8]{0:T(128)S(1)} all-reduce(f32[8]{0:T(128)S(1)} %multiply_reduce_fusion), channel_id=1, replica_groups=mesh['sub'=8,'grp'=4] {'sub','grp'}, use_global_device_ids=true, to_apply=%region_6.7 | all-reduce | flops 8 | bytes 64 | tf_op jit(solution)/shard_map/psum | solution.py:83
  222.9 6.6 %collective-permute-done.5 = f32[8,1,128]{2,0,1:T(8,128)S(1)} collective-permute-done((f32[8,1,128]{2,0,1:T(8,128)S(1)}, f32[8,1,128]{2,0,1:T(8,128)S(1)}, u32[]{:S(2)}, u32[]{:S(2)}) %collective-permute-start.5) | collective-permute-done | bytes 4128 | tf_op jit(solution)/shard_map/ppermute | solution.py:29
  229.5 0.3 convolution_bitcast_fusion.1
  229.9 37.4 %all_gather.11 = f32[8,4096]{1,0:T(8,128)S(1)} all-gather(f32[8,128]{1,0:T(8,128)S(1)} %reshape.76), channel_id=1, replica_groups=mesh['sub'=8,'grp'=4] {'sub','grp'}, dimensions={1}, use_global_device_ids=true | all-gather | bytes 135168 | tf_op jit(solution)/shard_map/all_gather | solution.py:65
  267.3 2.7 fusion.51
  270.1 0.5 collective-permute-start.6
  270.6 2.5 fusion.6
  273.1 3.7 collective-permute-done.6
  276.9 1.0 fusion
  277.9 1.4 collective-permute-start.7
  279.3 0.7 scatter_custom_fusion
  280.0 0.6 collective-permute-done.7
  280.8 5.8 %psum.60 = f32[8]{0:T(128)S(1)} all-reduce(f32[8]{0:T(128)S(1)} %fusion.17), channel_id=1, replica_groups=mesh['sub'=8,'grp'=4] {'grp'}, use_global_device_ids=true, to_apply=%region_8.9 | all-reduce | flops 8 | bytes 64 | tf_op jit(solution)/shard_map/psum | solution.py:20
  286.5 22.9 %psum.61 = f32[8]{0:T(128)S(1)} all-reduce(f32[8]{0:T(128)S(1)} %psum.60), channel_id=1, replica_groups=mesh['sub'=8,'grp'=4] {'sub'}, use_global_device_ids=true, to_apply=%region_9.10 | all-reduce | flops 8 | bytes 64 | tf_op jit(solution)/shard_map/psum | solution.py:20
  309.4 1.5 fusion.4
  311.0 0.8 copy.81
  311.9 1.5 gather_fusion
  313.4 0.2 copy.82
  313.7 0.7 reshape.100
  314.4 2.6 all-to-all-start
  317.0 1.4 copy.88
  318.4 1.4 copy.89
  319.8 4.5 %all-to-all-done = f32[32,1,256]{2,1,0:T(1,128)S(1)} async-done(((f32[32,1,256]{2,1,0:T(1,128)}), f32[32,1,256]{2,1,0:T(1,128)S(1)}, u32[]{:S(2)}, u32[]{:S(2)}) %all-to-all-start) | async-done | bytes 32800 | tf_op jit(solution)/shard_map/all_to_all | solution.py:124
  324.3 0.5 broadcast.116
  324.8 0.7 reduce.6
  325.7 0.5 convolution_bitcast_fusion
  326.3 38.3 %psum.62 = f32[256,8]{0,1:T(8,128)S(1)} all-reduce(f32[256,8]{0,1:T(8,128)S(1)} %convolution_bitcast_fusion), channel_id=1, replica_groups=mesh['sub'=8,'grp'=4] {'sub','grp'}, use_global_device_ids=true, to_apply=%region_11.12 | all-reduce | flops 2048 | bytes 16384 | tf_op jit(solution)/shard_map/psum | solution.py:128
  364.5 1.0 convolution_subtract_fusion
  365.5 0.2 fusion.52
  365.6 40.1 %psum.63 = f32[8,8]{0,1:T(8,128)S(1)} all-reduce(f32[8,8]{0,1:T(8,128)S(1)} %fusion.52), channel_id=1, replica_groups=mesh['sub'=8,'grp'=4] {'sub','grp'}, use_global_device_ids=true, to_apply=%region_12.13 | all-reduce | flops 64 | bytes 512 | tf_op jit(solution)/shard_map/psum | solution.py:133
  405.8 0.7 cholesky.18
  406.5 0.6 compare_reduce_fusion
  407.2 0.6 select_bitcast_fusion
  407.8 0.6 custom-call.7
  408.5 0.9 convolution_multiply_fusion
  409.3 0.7 copy.90
  (73 shorter events, 1.9 us)
Async XLA Ops:
  0.6 51.1 %copy-start = (f32[2,512,512]{2,1,0:T(8,128)S(1)}, f32[2,512,512]{2,1,0:T(8,128)}, u32[]{:S(2)}) copy-start(f32[2,512,512]{2,1,0:T(8,128)} %param.10) | copy-start | bytes 6291460
  0.6 2.7 copy-start.6
  0.7 2.7 copy-start.7
  0.7 2.6 copy-start.5
  0.7 2.7 copy-start.2
  2.2 1.1 copy-start.9
  2.2 1.1 copy-start.10
  48.9 1.4 copy-start.1
  51.4 6.7 %collective-permute-start = (f32[8,32]{1,0:T(8,128)S(1)}, f32[8,32]{1,0:T(8,128)S(1)}, u32[]{:S(2)}, u32[]{:S(2)}) collective-permute-start(f32[8,32]{1,0:T(8,128)S(1)} %slice.79), channel_id=1, source_target_pairs={{0,1},{1,2},{2,3},{3,4},{4,5},{5,6},{6,7},{7,8},{8,9},{9,10},{10,1... | collective-permute-start | bytes 3080 | tf_op jit(solution)/shard_map/ppermute | solution.py:29
  58.4 2.0 collective-permute-start.1
  60.4 6.6 %collective-permute-start.2 = (f32[8,1,128]{2,0,1:T(8,128)S(1)}, f32[8,1,128]{2,0,1:T(8,128)S(1)}, u32[]{:S(2)}, u32[]{:S(2)}) collective-permute-start(f32[8,1,128]{2,0,1:T(8,128)S(1)} %get-tuple-element.32), channel_id=1, source_target_pairs={{0,1},{1,2},{2,3},{3,4},{4,5},{5,6},{6,7},{7,8},{8,9},{9,10},{10,1... | collective-permute-start | bytes 12296 | tf_op jit(solution)/shard_map/ppermute | solution.py:29
  106.9 6.6 %collective-permute-start.3 = (f32[8,32]{1,0:T(8,128)S(1)}, f32[8,32]{1,0:T(8,128)S(1)}, u32[]{:S(2)}, u32[]{:S(2)}) collective-permute-start(f32[8,32]{1,0:T(8,128)S(1)} %slice.86), channel_id=1, source_target_pairs={{0,1},{1,2},{2,3},{3,4},{4,5},{5,6},{6,7},{7,8},{8,9},{9,10},{10,1... | collective-permute-start | bytes 3080 | tf_op jit(solution)/shard_map/ppermute | solution.py:29
  113.8 2.0 collective-permute-start.4
  222.9 6.6 %collective-permute-start.5 = (f32[8,1,128]{2,0,1:T(8,128)S(1)}, f32[8,1,128]{2,0,1:T(8,128)S(1)}, u32[]{:S(2)}, u32[]{:S(2)}) collective-permute-start(f32[8,1,128]{2,0,1:T(8,128)S(1)} %get-tuple-element.30), channel_id=1, source_target_pairs={{0,1},{1,2},{2,3},{3,4},{4,5},{5,6},{6,7},{7,8},{8,9},{9,10},{10,1... | collective-permute-start | bytes 12296 | tf_op jit(solution)/shard_map/ppermute | solution.py:29
  267.3 12.0 %copy-start.11 = (s32[32]{0:T(128)S(1)}, s32[32]{0:T(128)}, u32[]{:S(2)}) copy-start(s32[32]{0:T(128)} %param.19) | copy-start | bytes 388
  270.1 6.8 %collective-permute-start.6 = (f32[8,32]{1,0:T(8,128)S(1)}, f32[8,32]{1,0:T(8,128)S(1)}, u32[]{:S(2)}, u32[]{:S(2)}) collective-permute-start(f32[8,32]{1,0:T(8,128)S(1)} %slice.93), channel_id=1, source_target_pairs={{0,1},{1,2},{2,3},{3,4},{4,5},{5,6},{6,7},{7,8},{8,9},{9,10},{10,1... | collective-permute-start | bytes 3080 | tf_op jit(solution)/shard_map/ppermute | solution.py:29
  273.1 52.7 %copy-start.3 = (f32[1024,256]{1,0:T(8,128)S(1)}, f32[1024,256]{1,0:T(8,128)}, u32[]{:S(2)}) copy-start(f32[1024,256]{1,0:T(8,128)} %param.18) | copy-start | bytes 3145732
  277.9 2.7 collective-permute-start.7
  310.9 2.5 copy-start.4
  314.4 9.8 %all-to-all-start = ((f32[32,1,256]{2,1,0:T(1,128)}), f32[32,1,256]{2,1,0:T(1,128)S(1)}, u32[]{:S(2)}, u32[]{:S(2)}) async-start(f32[32,1,256]{2,1,0:T(1,128)} %reshape.100), calls=%async_computation | async-start | bytes 65536 | tf_op jit(solution)/shard_map/all_to_all | solution.py:124
  364.5 45.5 %copy-start.8 = (f32[256,8]{0,1:T(8,128)}, f32[256,8]{0,1:T(8,128)S(1)}, u32[]{:S(2)}) copy-start(f32[256,8]{0,1:T(8,128)S(1)} %psum.62) | copy-start | bytes 24580
